TPU v7x, 32 devices: a whole 2x2x4 slice. The times are simulated.
32 devices in a mesh: chain: 16 (over z, y, x), grp: 2 (over core).
Axes of the slice: x: 2, y: 2, z: 4, core: 2. Of those that a mesh axis runs over, the one named last changes fastest.
Arguments:
- codes: bfloat16 [2, 16384, 6144], P(None, ('chain', 'grp')), may hold values from -6 to 6
- exponents: int32 [2, 512, 6144], P(None, ('chain', 'grp')), may hold values from -2 to 2
- column_map: int32 [32], replicated, may hold values from 0 to 31, each once
- row_order: int32 [32], replicated, may hold values from 0 to 31, each once
Outputs:
- rollout: bfloat16 [2, 6144, 16384], P(None, ('chain', 'grp'))
- block_sums: float32 [2, 6144, 512], P(None, ('chain', 'grp'))
All inputs are finite; a program needn't handle non-finite values.
Results may differ from a plain program's by a relative error of at most 0.001.
Values may be sent and summed in bfloat16 or wider, within the bound.
No kernel may reach another device: no remote copies, remote signals or barrier semaphores. Data moves between devices by JAX's collectives and lax.ppermute only.
A program may use at most 128 MiB of HBM per device.

v0:
```python
import jax
import jax.numpy as jnp
from jax import lax
from jax.sharding import PartitionSpec as P


def arrange(array, column_map, devices, col_width):
    layer_count, row_count, _ = array.shape
    order = (
        jnp.arange(col_width, dtype=jnp.int32)[:, None] + column_map[None, :] * col_width
    ).reshape(-1)
    picked = jnp.take(array, order, axis=2)
    return jnp.swapaxes(picked, 1, 2).reshape(layer_count, col_width, devices, row_count)


def shards(codes, exponents, column_map, row_order):
    chain_size = lax.axis_size("chain")
    grp_size = lax.axis_size("grp")
    devices = chain_size * grp_size
    layer_count, row_count, width_all = codes.shape
    col_width = width_all // devices
    scaling = jnp.exp2(exponents.astype(jnp.float32))
    values = (codes.astype(jnp.float32) * jnp.repeat(scaling, 32, axis=1)).astype(jnp.bfloat16)
    outgoing = arrange(values, column_map, devices, col_width)
    width = outgoing.shape[3]
    shaped = outgoing.reshape(layer_count, col_width, chain_size, grp_size, width)
    arrived = lax.all_to_all(
        lax.all_to_all(shaped, "chain", split_axis=2, concat_axis=2, tiled=True),
        "grp",
        split_axis=3,
        concat_axis=3,
        tiled=True,
    )
    arrived = arrived.reshape(layer_count, col_width, devices, width)
    values = arrived
    values = jnp.take(values, row_order, axis=2)
    rollout = values.reshape(layer_count, col_width, devices * row_count)
    block_sums = (
        rollout.astype(jnp.float32)
        .reshape(layer_count, col_width, devices * row_count // 32, 32)
        .sum(axis=-1)
    )
    return (rollout, block_sums)


def solution(mesh):
    return jax.shard_map(
        shards,
        mesh=mesh,
        in_specs=(P(None, ("chain", "grp"), None), P(None, ("chain", "grp"), None), P(), P()),
        out_specs=(P(None, ("chain", "grp"), None), P(None, ("chain", "grp"), None)),
        check_vma=False,
    )
```

profile of v0, /device:TPU:29, one launch (start us, length us, event | category | flops | bytes accessed | tf_op | source)
XLA Modules:
  0.0 540.0 jit_solution(8782882133313919337)
XLA Ops:
  0.6 0.7 broadcast_multiply_fusion
  1.3 0.1 add.66
  1.4 0.1 add.63
  1.6 1.2 multiply_exponential_fusion
  2.8 11.6 %fusion = bf16[2,512,6144]{2,1,0:T(8,128)(2,1)} fusion(bf16[2,512,6144]{2,1,0:T(8,128)(2,1)} %param.4, f32[2,16,6144]{2,1,0:T(8,128)S(1)} %multiply_exponential_fusion), kind=kLoop, calls=%fused_computation.4 | loop fusion | flops 18874368 | bytes 25952256 | tf_op jit(solution)/shard_map/convert_element_type | solution.py:23
  14.5 31.0 %copy.26 = bf16[2,512,6144]{1,0,2:T(2,128)(2,1)} copy(bf16[2,512,6144]{2,1,0:T(8,128)(2,1)} %fusion) | data formatting | bytes 25165824 | tf_op jit(solution)/shard_map/convert_element_type | solution.py:23
  45.4 67.6 %gather_fusion = bf16[6144,2,512]{2,1,0:T(2,128)(2,1)} fusion(bf16[2,512,6144]{1,0,2:T(2,128)(2,1)} %copy.26, s32[6144]{0:T(1024)S(1)} %broadcast_clamp_fusion), kind=kCustom, calls=%fused_computation | custom fusion | bytes 25190400 | tf_op jit(solution)/shard_map/jit(_take)/gather | solution.py:12
  113.0 23.6 %broadcast_select_fusion = bf16[6144,2,512]{2,1,0:T(2,128)(2,1)S(1)} fusion(bf16[6144,2,512]{2,1,0:T(2,128)(2,1)} %gather_fusion, pred[6144]{0:T(1024)(128)(4,1)S(1)} %compare_and_fusion), kind=kLoop, calls=%fused_computation.5 | loop fusion | flops 6291456 | bytes 25171968 | tf_op jit(solution)/shard_map/jit(_take)/select_n | solution.py:12
  136.6 10.1 %copy.27 = bf16[2,192,16,2,512]{4,0,3,1,2:T(2,128)(2,1)} copy(bf16[2,192,16,2,512]{4,0,3,2,1:T(2,128)(2,1)S(1)} %bitcast.21) | data formatting | bytes 25165824 | tf_op jit(solution)/shard_map/reshape;reshape | solution.py:26
  146.8 0.0 copy-start
  146.8 6.5 %all-to-all-start = ((bf16[2,192,16,2,512]{4,0,3,1,2:T(2,128)(2,1)}), bf16[2,192,16,2,512]{4,0,3,1,2:T(2,128)(2,1)}, u32[]{:S(2)}, u32[]{:S(2)}) async-start(bf16[2,192,16,2,512]{4,0,3,1,2:T(2,128)(2,1)} %copy.27), calls=%async_computation | async-start | bytes 25165824 | tf_op jit(solution)/shard_map/all_to_all | solution.py:28
  153.3 0.0 copy-done
  153.3 0.1 broadcast_in_dim.47
  153.4 0.1 broadcast_in_dim.48
  153.5 0.1 broadcast_bitcast_fusion
  153.6 285.1 %all-to-all-done = bf16[2,192,16,2,512]{4,0,3,1,2:T(2,128)(2,1)} async-done(((bf16[2,192,16,2,512]{4,0,3,1,2:T(2,128)(2,1)}), bf16[2,192,16,2,512]{4,0,3,1,2:T(2,128)(2,1)}, u32[]{:S(2)}, u32[]{:S(2)}) %all-to-all-start) | async-done | bytes 12582944 | tf_op jit(solution)/shard_map/all_to_all | solution.py:28
  438.7 13.3 %copy.28 = bf16[2,192,16,2,512]{4,0,2,1,3:T(2,128)(2,1)S(1)} copy(bf16[2,192,16,2,512]{4,0,3,1,2:T(2,128)(2,1)} %all-to-all-done) | data formatting | bytes 25165824 | tf_op jit(solution)/shard_map/all_to_all | solution.py:28
  452.0 15.3 %all_to_all.10 = bf16[2,192,16,2,512]{4,0,2,1,3:T(2,128)(2,1)S(1)} all-to-all(bf16[2,192,16,2,512]{4,0,2,1,3:T(2,128)(2,1)S(1)} %copy.28), channel_id=1, replica_groups=mesh['chain'=16,'grp'=2] {'grp'}, dimensions={3} | all-to-all | bytes 25165824 | tf_op jit(solution)/shard_map/all_to_all | solution.py:27
  467.3 10.0 %copy.34 = bf16[2,192,16,2,512]{4,1,0,3,2:T(8,128)(2,1)} copy(bf16[2,192,16,2,512]{4,0,2,1,3:T(2,128)(2,1)S(1)} %all_to_all.10) | data formatting | bytes 25165824 | tf_op jit(solution)/shard_map/reshape | solution.py:34
  477.3 11.4 %gather_fusion.1 = bf16[32,2,192,512]{3,2,1,0:T(8,128)(2,1)} fusion(bf16[2,192,32,512]{3,1,0,2:T(8,128)(2,1)} %bitcast.22, s32[1024]{0:T(1024)S(1)} %pad_clamp_fusion), kind=kCustom, calls=%fused_computation.1 | custom fusion | bytes 25165952 | tf_op jit(solution)/shard_map/jit(_take)/gather | solution.py:36
  488.7 10.6 %copy.35 = bf16[32,2,24,8,512]{4,3,0,2,1:T(8,128)(2,1)} copy(bf16[32,2,24,8,512]{4,3,2,1,0:T(8,128)(2,1)} %bitcast.17) | data formatting | bytes 25165824 | tf_op jit(solution)/shard_map/jit(_take)/gather | solution.py:36
  499.3 19.5 %copy.32 = bf16[2,192,32,512]{1,3,2,0:T(8,128)(2,1)} copy(bf16[2,192,32,512]{3,1,0,2:T(8,128)(2,1)} %bitcast.18) | data formatting | bytes 25165824 | tf_op jit(solution)/shard_map/jit(_take)/gather | solution.py:36
  518.8 9.2 %convert_reduce_fusion = f32[2,192,512]{1,2,0:T(8,128)S(1)} fusion(bf16[2,192,512,32]{1,3,2,0:T(8,128)(2,1)} %bitcast.19, pred[512]{0:T(512)(128)(4,1)S(1)} %broadcast_in_dim.48), kind=kLoop, calls=%fused_computation.2 | loop fusion | flops 18677760 | bytes 13369856 | tf_op jit(solution)/shard_map/reduce_sum | solution.py:41
  528.1 1.2 copy.33
  529.3 10.7 %broadcast_select_fusion.1 = bf16[2,192,16384]{2,1,0:T(8,128)(2,1)} fusion(bf16[2,192,16384]{2,1,0:T(8,128)(2,1)} %bitcast.20, pred[16384]{0:T(1024)(128)(4,1)S(1)} %bitcast.24), kind=kLoop, calls=%fused_computation.6 | loop fusion | flops 6291456 | bytes 25182208 | tf_op jit(solution)/shard_map/jit(_take)/select_n | solution.py:36
  (8 shorter events, 0.1 us)
Async XLA Ops:
  146.8 6.5 %copy-start = (s32[32]{0:T(128)S(1)}, s32[32]{0:T(128)}, u32[]{:S(2)}) copy-start(s32[32]{0:T(128)} %param.7) | copy-start | bytes 388
  146.8 291.9 %all-to-all-start = ((bf16[2,192,16,2,512]{4,0,3,1,2:T(2,128)(2,1)}), bf16[2,192,16,2,512]{4,0,3,1,2:T(2,128)(2,1)}, u32[]{:S(2)}, u32[]{:S(2)}) async-start(bf16[2,192,16,2,512]{4,0,3,1,2:T(2,128)(2,1)} %copy.27), calls=%async_computation | async-start | bytes 25165824 | tf_op jit(solution)/shard_map/all_to_all | solution.py:28
where the time goes:
time: 542 us; the launch traced here: 540 us
  waiting for transfers between devices  285 us (53%)
  local copies, waits for them, and re-layouts  175 us (32%)
  other arithmetic  57.2 us (11%)
  blocking collectives  15.3 us (3%)
  starting transfers between devices  6.52 us (1%)
    all_to_all x1, waiting for transfers between devices, shards(): lax.all_to_all(shaped, 'chain', split_axis=2, concat_axis=2, tiled=True)  285 us
    gather x1, local copies, waits for them, and re-layouts, arrange(): picked = jnp.take(array, order, axis=2)  67.6 us
    gather x3, local copies, waits for them, and re-layouts, shards(): values = jnp.take(values, row_order, axis=2)  41.5 us
    convert_element_type x1, local copies, waits for them, and re-layouts, shards(): (codes.astype(jnp.float32) * jnp.repeat(scaling, 32, axis=1)).astype(jnp....  31 us
    select_n x2, other arithmetic, arrange(): picked = jnp.take(array, order, axis=2)  23.6 us
    all_to_all x1, blocking collectives, shards(): lax.all_to_all(lax.all_to_all(shaped, 'chain', split_axis=2, concat_axis=...  15.3 us
    all_to_all x1, local copies, waits for them, and re-layouts, shards(): lax.all_to_all(shaped, 'chain', split_axis=2, concat_axis=2, tiled=True)  13.3 us
    convert_element_type x1, other arithmetic, shards(): (codes.astype(jnp.float32) * jnp.repeat(scaling, 32, axis=1)).astype(jnp....  11.6 us
  transfers between devices with their start and end apart: 1, of which 1 were waited for; matrix products, arithmetic and copies ran while one was open for 0% of the time, Pallas kernels for 0%

commit v1 on v0

v1 whole, which is shorter than its diff:
```python
import functools
import math

import jax
import jax.numpy as jnp
from jax import lax
from jax.experimental import pallas as pl
from jax.experimental.pallas import tpu as pltpu
from jax.sharding import PartitionSpec as P

AXES = ("chain", "grp")
BLOCK = 32
LANES = 128


def arrange(array, column_map, devices, col_width):
    layer_count, row_count, _ = array.shape
    order = (
        jnp.arange(col_width, dtype=jnp.int32)[:, None] + column_map[None, :] * col_width
    ).reshape(-1)
    picked = jnp.take(array, order, axis=2)
    return jnp.swapaxes(picked, 1, 2).reshape(layer_count, col_width, devices, row_count)


def plain(codes, exponents, column_map, row_order):
    chain_size = lax.axis_size("chain")
    grp_size = lax.axis_size("grp")
    devices = chain_size * grp_size
    layer_count, row_count, width_all = codes.shape
    col_width = width_all // devices
    scaling = jnp.exp2(exponents.astype(jnp.float32))
    values = (codes.astype(jnp.float32) * jnp.repeat(scaling, BLOCK, axis=1)).astype(jnp.bfloat16)
    outgoing = arrange(values, column_map, devices, col_width)
    shaped = outgoing.reshape(layer_count, col_width, chain_size, grp_size, row_count)
    arrived = lax.all_to_all(
        lax.all_to_all(shaped, "chain", split_axis=2, concat_axis=2, tiled=True),
        "grp",
        split_axis=3,
        concat_axis=3,
        tiled=True,
    )
    arrived = arrived.reshape(layer_count, col_width, devices, row_count)
    rollout = jnp.take(arrived, row_order, axis=2).reshape(layer_count, col_width, devices * row_count)
    block_sums = (
        rollout.astype(jnp.float32)
        .reshape(layer_count, col_width, devices * row_count // BLOCK, BLOCK)
        .sum(axis=-1)
    )
    return rollout, block_sums


def pack_kernel(where_ref, codes_ref, exponents_ref, out_ref, turned, *, col_width, group):
    member = pl.program_id(1)
    rows = codes_ref.shape[1]

    @pl.when(member == 0)
    def _():
        scaling = jnp.exp2(exponents_ref[0].astype(jnp.float32)).astype(jnp.bfloat16)
        for tile in range(col_width * group // LANES):
            lanes = slice(tile * LANES, (tile + 1) * LANES)
            parts = [
                codes_ref[0, b * BLOCK : (b + 1) * BLOCK, lanes] * scaling[b : b + 1, lanes]
                for b in range(rows // BLOCK)
            ]
            turned[lanes, :] = jnp.concatenate(parts, axis=0).T

    out_ref[0] = turned[pl.ds(pl.multiple_of(member * col_width, 16), col_width), :]


def pack(codes, exponents, where, layer, devices):
    _, rows, width_all = codes.shape
    col_width = width_all // devices
    group = math.lcm(col_width, LANES) // col_width
    wide = col_width * group
    return pl.pallas_call(
        functools.partial(pack_kernel, col_width=col_width, group=group),
        grid_spec=pltpu.PrefetchScalarGridSpec(
            num_scalar_prefetch=1,
            grid=(devices // group, group),
            in_specs=[
                pl.BlockSpec((1, rows, wide), lambda g, m, where: (layer, 0, g)),
                pl.BlockSpec((1, rows // BLOCK, wide), lambda g, m, where: (layer, 0, g)),
            ],
            out_specs=pl.BlockSpec(
                (1, col_width, rows), lambda g, m, where: (where[g * group + m], 0, 0)
            ),
            scratch_shapes=[pltpu.VMEM((wide, rows), jnp.bfloat16)],
        ),
        out_shape=jax.ShapeDtypeStruct((devices, col_width, rows), jnp.bfloat16),
        name=f"pack{layer}",
    )(where, codes, exponents)


def place_kernel(order_ref, *refs, take, rows):
    pieces, (rollout_ref, sums_ref) = refs[:take], refs[-2:]
    blocks = rows // BLOCK
    source = lax.broadcasted_iota(jnp.int32, (rows, take * blocks), 0) // BLOCK
    target = lax.broadcasted_iota(jnp.int32, (rows, take * blocks), 1)
    total = None
    for k, piece in enumerate(pieces):
        values = piece[0]
        rollout_ref[0, :, k * rows : (k + 1) * rows] = values
        mask = (source + k * blocks == target).astype(jnp.bfloat16)
        part = jnp.dot(values, mask, preferred_element_type=jnp.float32)
        total = part if total is None else total + part
    sums_ref[0] = total


def place(arrived, order, layer, layer_count, previous):
    devices, col_width, rows = arrived.shape
    take = LANES * BLOCK // rows
    piece = lambda k: pl.BlockSpec(
        (1, col_width, rows), lambda s, order: (order[s * take + k], 0, 0)
    )
    carried = [] if previous is None else list(previous)
    return pl.pallas_call(
        functools.partial(place_kernel, take=take, rows=rows),
        grid_spec=pltpu.PrefetchScalarGridSpec(
            num_scalar_prefetch=1,
            grid=(devices // take,),
            in_specs=[piece(k) for k in range(take)]
            + [pl.BlockSpec(memory_space=pl.ANY)] * len(carried),
            out_specs=[
                pl.BlockSpec((1, col_width, take * rows), lambda s, order: (layer, 0, s)),
                pl.BlockSpec((1, col_width, LANES), lambda s, order: (layer, 0, s)),
            ],
        ),
        out_shape=[
            jax.ShapeDtypeStruct((layer_count, col_width, devices * rows), jnp.bfloat16),
            jax.ShapeDtypeStruct((layer_count, col_width, devices * rows // BLOCK), jnp.float32),
        ],
        input_output_aliases={1 + take + i: i for i in range(len(carried))},
        name=f"place{layer}",
    )(order, *[arrived] * take, *carried)


def shards(codes, exponents, column_map, row_order):
    devices = lax.axis_size("chain") * lax.axis_size("grp")
    layer_count, rows, width_all = codes.shape
    col_width = width_all // devices
    whole_tiles = (
        rows % LANES == 0
        and LANES * BLOCK % rows == 0
        and devices % (LANES * BLOCK // rows) == 0
        and col_width % 16 == 0
        and devices % (math.lcm(col_width, LANES) // col_width) == 0
    )
    if not whole_tiles:
        return plain(codes, exponents, column_map, row_order)
    where = jnp.sum(
        jnp.where(
            column_map[None, :] == jnp.arange(devices, dtype=jnp.int32)[:, None],
            jnp.arange(devices, dtype=jnp.int32)[None, :],
            0,
        ),
        axis=1,
        dtype=jnp.int32,
    )
    arrived = [
        lax.all_to_all(
            pack(codes, exponents, where, layer, devices), AXES, split_axis=0, concat_axis=0, tiled=True
        )
        for layer in range(layer_count)
    ]
    done = None
    for layer in range(layer_count):
        done = place(arrived[layer], row_order, layer, layer_count, done)
    return tuple(done)


def solution(mesh):
    return jax.shard_map(
        shards,
        mesh=mesh,
        in_specs=(P(None, AXES, None), P(None, AXES, None), P(), P()),
        out_specs=(P(None, AXES, None), P(None, AXES, None)),
        check_vma=False,
    )
```

time: 542 us -> 324 us (0.60)
  local copies, waits for them, and re-layouts: 175 us -> 0 us
  Pallas kernels: 0 us -> 60.9 us
  other arithmetic: 57.2 us -> 1.28 us
  waiting for transfers between devices: 285 us -> 242 us
  blocking collectives: 15.3 us -> 0 us
  starting transfers between devices: 6.52 us -> 13.1 us
    gather x4 -> x0, local copies, waits for them, and re-layouts: 109 us -> none  [the longest x1 67.6 us: arrange(): picked = jnp.take(array, order, axis=2)]
    pallas_call x0 -> x4, Pallas kernels: none -> 60.9 us  [the longest x2 45.4 us: pack(): pl.pallas_call(functools.partial(pack_kernel, col_width=col_width, group=...]
    all_to_all x1 -> x2, waiting for transfers between devices: 285 us -> 242 us  [shards(): lax.all_to_all(pack(codes, exponents, where, layer, devices), AXES, split...]
    select_n x4 -> x0, other arithmetic: 34.3 us -> none  [the longest x2 23.6 us: arrange(): picked = jnp.take(array, order, axis=2)]
    convert_element_type x1 -> x0, local copies, waits for them, and re-layouts: 31 us -> none  [shards(): (codes.astype(jnp.float32) * jnp.repeat(scaling, 32, axis=1)).astype(jnp....]
    all_to_all x1 -> x0, blocking collectives: 15.3 us -> none  [shards(): lax.all_to_all(lax.all_to_all(shaped, 'chain', split_axis=2, concat_axis=...]
    all_to_all x1 -> x0, local copies, waits for them, and re-layouts: 13.3 us -> none  [shards(): lax.all_to_all(shaped, 'chain', split_axis=2, concat_axis=2, tiled=True)]
    convert_element_type x1 -> x0, other arithmetic: 11.6 us -> none  [shards(): (codes.astype(jnp.float32) * jnp.repeat(scaling, 32, axis=1)).astype(jnp....]
  transfers between devices with their start and end apart: 1 -> 2, of which waited for: 1 -> 2; matrix products, arithmetic and copies ran while one was open for 0% -> 0% of each run, Pallas kernels for 0% -> 10%
where the time goes in v1:
time: 324 us; the launch traced here: 318 us
  waiting for transfers between devices  242 us (75%)
  Pallas kernels  60.9 us (19%)
  starting transfers between devices  13.1 us (4%)
    all_to_all x2, waiting for transfers between devices, shards(): lax.all_to_all(pack(codes, exponents, where, layer, devices), AXES, split...  242 us
    pallas_call x2, Pallas kernels, pack(): pl.pallas_call(functools.partial(pack_kernel, col_width=col_width, group=...  45.4 us
    pallas_call x2, Pallas kernels, place(): pl.pallas_call(functools.partial(place_kernel, take=take, rows=rows), gri...  15.5 us
    all_to_all x2, starting transfers between devices, shards(): lax.all_to_all(pack(codes, exponents, where, layer, devices), AXES, split...  13.1 us
  transfers between devices with their start and end apart: 2, of which 2 were waited for; matrix products, arithmetic and copies ran while one was open for 0% of the time, Pallas kernels for 10%

profile of v1, /device:TPU:29, one launch (start us, length us, event | category | flops | bytes accessed | tf_op | source)
XLA Modules:
  0.0 318.2 jit_solution(11448167630518745485)
XLA Ops:
  0.6 1.3 select_reduce_fusion.where_ref
  1.9 22.7 %pack0.1 = bf16[32,192,512]{2,1,0:T(8,128)(2,1)} custom-call(s32[32]{0:T(128)} %select_reduce_fusion.where_ref, bf16[2,512,6144]{2,1,0:T(8,128)(2,1)} %codes_ref.3, s32[2,16,6144]{2,1,0:T(8,128)} %exponents_ref.3), custom_call_target="tpu_custom_call" | custom-call | tf_op jit(solution)/shard_map/pack0/pallas_call | solution.py:75
  24.6 6.2 %all-to-all-start.1 = ((bf16[32,192,512]{2,1,0:T(8,128)(2,1)}), bf16[32,192,512]{2,1,0:T(8,128)(2,1)}, u32[]{:S(2)}, u32[]{:S(2)}) async-start(bf16[32,192,512]{2,1,0:T(8,128)(2,1)} %pack0.1), calls=%async_computation.1 | async-start | bytes 12582912 | tf_op jit(solution)/shard_map/all_to_all | solution.py:160
  30.8 22.7 %pack1.1 = bf16[32,192,512]{2,1,0:T(8,128)(2,1)} custom-call(s32[32]{0:T(128)} %select_reduce_fusion.where_ref, bf16[2,512,6144]{2,1,0:T(8,128)(2,1)} %codes_ref.3, s32[2,16,6144]{2,1,0:T(8,128)} %exponents_ref.3), custom_call_target="tpu_custom_call" | custom-call | tf_op jit(solution)/shard_map/pack1/pallas_call | solution.py:75
  53.5 113.7 %all-to-all-done.1.refs_0_.refs_1_.refs_2_.refs_3_.refs_4_.refs_5_.refs_6_.refs_7_ = bf16[32,192,512]{2,1,0:T(8,128)(2,1)} async-done(((bf16[32,192,512]{2,1,0:T(8,128)(2,1)}), bf16[32,192,512]{2,1,0:T(8,128)(2,1)}, u32[]{:S(2)}, u32[]{:S(2)}) %all-to-all-start.1) | async-done | bytes 6291488 | tf_op jit(solution)/shard_map/all_to_all | solution.py:160
  167.2 7.0 %all-to-all-start = ((bf16[32,192,512]{2,1,0:T(8,128)(2,1)}), bf16[32,192,512]{2,1,0:T(8,128)(2,1)}, u32[]{:S(2)}, u32[]{:S(2)}) async-start(bf16[32,192,512]{2,1,0:T(8,128)(2,1)} %pack1.1), calls=%async_computation | async-start | bytes 12582912 | tf_op jit(solution)/shard_map/all_to_all | solution.py:160
  174.2 7.7 %place0.1 = (bf16[2,192,16384]{2,1,0:T(8,128)(2,1)}, f32[2,192,512]{2,1,0:T(8,128)}) custom-call(s32[32]{0:T(128)} %order_ref.3, bf16[32,192,512]{2,1,0:T(8,128)(2,1)} %all-to-all-done.1.refs_0_.refs_1_.refs_2_.refs_3_.refs_4_.refs_5_.refs_6_.refs_7_, bf16[32,192,512]{2,1,0:T(8,128)(2,1)} %all-to-all-done.1.refs_0_.refs_1_.refs_2_.refs_3_.refs_4_.refs_5_.refs_6_.refs_7_, ...), custom_call_target="tpu_custom_call" | custom-call | tf_op jit(solution)/shard_map/place0/pallas_call | solution.py:116
  181.9 128.6 %all-to-all-done.refs_0_.refs_1_.refs_2_.refs_3_.refs_4_.refs_5_.refs_6_.refs_7_ = bf16[32,192,512]{2,1,0:T(8,128)(2,1)} async-done(((bf16[32,192,512]{2,1,0:T(8,128)(2,1)}), bf16[32,192,512]{2,1,0:T(8,128)(2,1)}, u32[]{:S(2)}, u32[]{:S(2)}) %all-to-all-start) | async-done | bytes 6291488 | tf_op jit(solution)/shard_map/all_to_all | solution.py:160
  310.5 7.7 %place1.1 = (bf16[2,192,16384]{2,1,0:T(8,128)(2,1)}, f32[2,192,512]{2,1,0:T(8,128)}) custom-call(s32[32]{0:T(128)} %order_ref.3, bf16[32,192,512]{2,1,0:T(8,128)(2,1)} %all-to-all-done.refs_0_.refs_1_.refs_2_.refs_3_.refs_4_.refs_5_.refs_6_.refs_7_, ...), custom_call_target="tpu_custom_call", output_to_operand_aliasing={{0}: (9, {}), {1}: (10, {})} | custom-call | tf_op jit(solution)/shard_map/place1/pallas_call | solution.py:116
Async XLA Ops:
  24.6 142.6 %all-to-all-start.1 = ((bf16[32,192,512]{2,1,0:T(8,128)(2,1)}), bf16[32,192,512]{2,1,0:T(8,128)(2,1)}, u32[]{:S(2)}, u32[]{:S(2)}) async-start(bf16[32,192,512]{2,1,0:T(8,128)(2,1)} %pack0.1), calls=%async_computation.1 | async-start | bytes 12582912 | tf_op jit(solution)/shard_map/all_to_all | solution.py:160
  167.2 143.3 %all-to-all-start = ((bf16[32,192,512]{2,1,0:T(8,128)(2,1)}), bf16[32,192,512]{2,1,0:T(8,128)(2,1)}, u32[]{:S(2)}, u32[]{:S(2)}) async-start(bf16[32,192,512]{2,1,0:T(8,128)(2,1)} %pack1.1), calls=%async_computation | async-start | bytes 12582912 | tf_op jit(solution)/shard_map/all_to_all | solution.py:160

commit v2 on v0

v2 whole, which is shorter than its diff:
```python
import functools
import itertools
import math

import jax
import jax.numpy as jnp
import numpy as np
from jax import lax
from jax.experimental import pallas as pl
from jax.experimental.pallas import tpu as pltpu
from jax.sharding import PartitionSpec as P


AXES = ("chain", "grp")
BLOCK = 32
LANES = 128


def arrange(array, column_map, devices, col_width):
    layer_count, row_count, _ = array.shape
    order = (
        jnp.arange(col_width, dtype=jnp.int32)[:, None] + column_map[None, :] * col_width
    ).reshape(-1)
    picked = jnp.take(array, order, axis=2)
    return jnp.swapaxes(picked, 1, 2).reshape(layer_count, col_width, devices, row_count)


def plain(codes, exponents, column_map, row_order):
    chain_size = lax.axis_size("chain")
    grp_size = lax.axis_size("grp")
    devices = chain_size * grp_size
    layer_count, row_count, width_all = codes.shape
    col_width = width_all // devices
    scaling = jnp.exp2(exponents.astype(jnp.float32))
    values = (codes.astype(jnp.float32) * jnp.repeat(scaling, BLOCK, axis=1)).astype(jnp.bfloat16)
    outgoing = arrange(values, column_map, devices, col_width)
    shaped = outgoing.reshape(layer_count, col_width, chain_size, grp_size, row_count)
    arrived = lax.all_to_all(
        lax.all_to_all(shaped, "chain", split_axis=2, concat_axis=2, tiled=True),
        "grp",
        split_axis=3,
        concat_axis=3,
        tiled=True,
    )
    arrived = arrived.reshape(layer_count, col_width, devices, row_count)
    rollout = jnp.take(arrived, row_order, axis=2).reshape(layer_count, col_width, devices * row_count)
    block_sums = (
        rollout.astype(jnp.float32)
        .reshape(layer_count, col_width, devices * row_count // BLOCK, BLOCK)
        .sum(axis=-1)
    )
    return rollout, block_sums


def places_of(mesh):
    spots = np.array([(*d.coords, d.core_on_chip) for d in mesh.devices.flat])
    spots -= spots.min(axis=0)
    sizes = spots.max(axis=0) + 1
    axes = sorted(range(3), key=lambda a: -sizes[a]) + [3]
    return spots[:, axes], sizes[axes]


def routes(mesh):
    spots, sizes = places_of(mesh)
    number = {tuple(spot): i for i, spot in enumerate(spots.tolist())}
    side = [
        offset
        for offset in itertools.product(*(range(n) for n in sizes[1:]))
    ]
    side.sort(key=lambda offset: (-sum(offset[:-1]), -offset[0], offset[-1]))
    length = int(sizes[0])

    def step(shift, offset):
        targets = []
        for spot in spots.tolist():
            far = shift(spot) if callable(shift) else shift
            moved = [(a + b) % n for a, b, n in zip(spot, (far, *offset), sizes.tolist())]
            targets.append(number[tuple(moved)])
        return targets

    steps = []
    half = [step(length // 2, o) for o in side] if length % 2 == 0 else []
    near = [step(0, o) for o in side if any(o)]
    for pair in itertools.zip_longest(half, near):
        steps += [p for p in pair if p is not None]
    for shift in range(1, (length + 1) // 2):
        for offset in side:
            for turn in (0, 1):
                steps.append(
                    step(lambda spot: shift if (spot[-1] + turn) % 2 == 0 else length - shift, offset)
                )
    target = np.array(steps, np.int32)
    return target, np.argsort(target, axis=1).astype(np.int32)


def pack_kernel(column_ref, *refs, windows, col_width, step):
    codes, exponents = refs[:windows], refs[windows : 2 * windows]
    out_ref, turned = refs[2 * windows :]
    rows = codes[0].shape[1]
    for tile, (code, exponent) in enumerate(zip(codes, exponents)):
        scaling = jnp.exp2(exponent[0].astype(jnp.float32)).astype(jnp.bfloat16)
        parts = [
            code[0, b * BLOCK : (b + 1) * BLOCK, :] * scaling[b : b + 1, :]
            for b in range(rows // BLOCK)
        ]
        turned[tile * LANES : (tile + 1) * LANES, :] = jnp.concatenate(parts, axis=0).T
    offset = lax.rem(column_ref[step] * col_width, LANES)
    out_ref[0] = turned[pl.ds(pl.multiple_of(offset, 16), col_width), :]


def pack(codes, exponents, column, step, devices):
    layer_count, rows, width_all = codes.shape
    col_width = width_all // devices
    windows = -(-(LANES - math.gcd(col_width, LANES) + col_width) // LANES)
    last = width_all // LANES - 1

    def window(height, tile):
        return pl.BlockSpec(
            (1, height, LANES),
            lambda layer, column: (
                layer, 0, jnp.minimum(lax.div(column[step] * col_width, LANES) + tile, last)
            ),
        )

    return pl.pallas_call(
        functools.partial(pack_kernel, windows=windows, col_width=col_width, step=step),
        grid_spec=pltpu.PrefetchScalarGridSpec(
            num_scalar_prefetch=1,
            grid=(layer_count,),
            in_specs=[window(rows, tile) for tile in range(windows)]
            + [window(rows // BLOCK, tile) for tile in range(windows)],
            out_specs=pl.BlockSpec((1, col_width, rows), lambda layer, column: (layer, 0, 0)),
            scratch_shapes=[pltpu.VMEM((windows * LANES, rows), jnp.bfloat16)],
        ),
        out_shape=jax.ShapeDtypeStruct((layer_count, col_width, rows), jnp.bfloat16),
    )(column, *[codes] * windows, *[exponents] * windows)


def place_kernel(spot_ref, *refs, steps, first):
    count = len(steps)
    pieces = refs[:count]
    rollout, sums, held, total, came, left, moved = refs[-7:]
    layers, _, rows = held.shape[1:]
    per_tile = LANES * BLOCK // rows
    arrivals = [pltpu.make_async_copy(pieces[k], held.at[k], came.at[k]) for k in range(count)]
    for copy in arrivals:
        copy.start()
    if first:
        total[...] = jnp.zeros_like(total)
    else:
        so_far = pltpu.make_async_copy(refs[count + 1], total, moved.at[0])
        so_far.start()
        so_far.wait()
    block = lax.broadcasted_iota(jnp.int32, (rows, LANES), 0) // BLOCK
    lane = lax.broadcasted_iota(jnp.int32, (rows, LANES), 1)
    leavings = []
    for k, step in enumerate(steps):
        spot = spot_ref[step]
        arrivals[k].wait()
        leaving = pltpu.make_async_copy(
            held.at[k], rollout.at[:, :, pl.ds(pl.multiple_of(spot * rows, LANES), rows)], left.at[k]
        )
        leaving.start()
        leavings.append(leaving)
        mask = (block + lax.rem(spot, per_tile) * (rows // BLOCK) == lane).astype(jnp.bfloat16)
        tile = pl.ds(pl.multiple_of(lax.div(spot, per_tile) * LANES, LANES), LANES)
        for layer in range(layers):
            total[layer, :, tile] += jnp.dot(held[k, layer], mask, preferred_element_type=jnp.float32)
    last = pltpu.make_async_copy(total, sums, moved.at[1])
    last.start()
    for copy in leavings:
        copy.wait()
    last.wait()


def place(pieces, steps, spot, devices, previous):
    layer_count, col_width, rows = pieces[0].shape
    count = len(pieces)
    carried = [] if previous is None else list(previous)
    whole = jax.ShapeDtypeStruct((layer_count, col_width, devices * rows), jnp.bfloat16)
    sums = jax.ShapeDtypeStruct((layer_count, col_width, devices * rows // BLOCK), jnp.float32)
    anywhere = pl.BlockSpec(memory_space=pl.ANY)
    return pl.pallas_call(
        functools.partial(place_kernel, steps=steps, first=previous is None),
        grid_spec=pltpu.PrefetchScalarGridSpec(
            num_scalar_prefetch=1,
            grid=(1,),
            in_specs=[anywhere] * (count + len(carried)),
            out_specs=[anywhere, anywhere],
            scratch_shapes=[
                pltpu.VMEM((count, layer_count, col_width, rows), jnp.bfloat16),
                pltpu.VMEM(sums.shape, jnp.float32),
                pltpu.SemaphoreType.DMA((count,)),
                pltpu.SemaphoreType.DMA((count,)),
                pltpu.SemaphoreType.DMA((2,)),
            ],
        ),
        out_shape=[whole, sums],
        input_output_aliases={1 + count + i: i for i in range(len(carried))},
    )(spot, *pieces, *carried)


def lookup(table, index):
    hit = index[:, None] == jnp.arange(table.shape[0], dtype=jnp.int32)[None, :]
    return jnp.sum(jnp.where(hit, table[None, :], 0), axis=1, dtype=jnp.int32)


def groups_of(steps):
    sizes, left = [], steps
    for size in (2, 2, 4, 8):
        if left > 2 * size:
            sizes.append(size)
            left -= size
    while left > 0:
        sizes.append(min(left, 8))
        left -= sizes[-1]
    ends = np.cumsum(sizes[::-1])
    return [list(range(end - size, end)) for end, size in zip(ends, sizes[::-1])]


def shards(target, source, codes, exponents, column_map, row_order):
    devices = lax.axis_size("chain") * lax.axis_size("grp")
    if not fits(codes.shape, devices):
        return plain(codes, exponents, column_map, row_order)
    steps = len(target)
    me = lax.axis_index("chain") * lax.axis_size("grp") + lax.axis_index("grp")
    mine = (jnp.arange(devices, dtype=jnp.int32) == me)[None, :]
    itself = jnp.full((1,), me, jnp.int32)
    to = jnp.concatenate([jnp.sum(jnp.where(mine, target, 0), axis=1, dtype=jnp.int32), itself])
    came = jnp.concatenate([jnp.sum(jnp.where(mine, source, 0), axis=1, dtype=jnp.int32), itself])
    column = lookup(column_map, to)
    hit = came[:, None] == row_order[None, :]
    spot = jnp.sum(
        jnp.where(hit, jnp.arange(devices, dtype=jnp.int32)[None, :], 0), axis=1, dtype=jnp.int32
    )
    arrived = []
    for step in range(steps):
        piece = pack(codes, exponents, column, step, devices)
        arrived.append(lax.ppermute(piece, AXES, list(enumerate(target[step].tolist()))))
    arrived.append(pack(codes, exponents, column, steps, devices))
    done = None
    for number, group in enumerate(groups_of(steps)):
        if number == 0:
            group = [steps, *group]
        done = place([arrived[k] for k in group], group, spot, devices, done)
    return tuple(done)


def fits(shape, devices):
    _, rows, width_all = shape
    return (
        rows % LANES == 0
        and LANES * BLOCK % rows == 0
        and devices % (LANES * BLOCK // rows) == 0
        and width_all // devices % 16 == 0
        and width_all % LANES == 0
    )


def solution(mesh):
    target, source = routes(mesh)
    return jax.shard_map(
        functools.partial(shards, target, source),
        mesh=mesh,
        in_specs=(P(None, AXES, None), P(None, AXES, None), P(), P()),
        out_specs=(P(None, AXES, None), P(None, AXES, None)),
        check_vma=False,
    )
```

time: 542 us -> 296 us (0.55)
  the two profiles are of different devices: /device:TPU:29 before, /device:TPU:7 now
where the time goes in v2:
time: 296 us; the launch traced here: 294 us
  Pallas kernels  115 us (39%)
  starting transfers between devices  102 us (34%)
  waiting for transfers between devices  70.9 us (24%)
  other arithmetic  3.63 us (1%)
    ppermute x31, starting transfers between devices, shards(): lax.ppermute(piece, AXES, list(enumerate(target[step].tolist())))  102 us
    pallas_call x32, Pallas kernels, pack(): pl.pallas_call(functools.partial(pack_kernel, windows=windows, col_width=...  86.5 us
    ppermute x31, waiting for transfers between devices, shards(): lax.ppermute(piece, AXES, list(enumerate(target[step].tolist())))  70.9 us
    pallas_call x6, Pallas kernels, place(): pl.pallas_call(functools.partial(place_kernel, steps=steps, first=previou...  28 us
  transfers between devices with their start and end apart: 31, of which 9 were waited for; matrix products, arithmetic and copies ran while one was open for 0% of the time, Pallas kernels for 37%

profile of v2, /device:TPU:7, one launch (start us, length us, event | category | flops | bytes accessed | tf_op | source)
XLA Modules:
  0.0 294.5 jit_solution(2481563150720769538)
XLA Ops:
  3.5 2.7 shard_map.102
  8.4 2.7 shard_map.103
  16.8 2.7 shard_map.105
  21.1 2.7 shard_map.106
  26.1 2.7 shard_map.107
  28.8 15.6 %collective-permute-done.24.refs_1_ = bf16[2,192,512]{2,1,0:T(8,128)(2,1)S(1)} collective-permute-done((bf16[2,192,512]{2,1,0:T(8,128)(2,1)}, bf16[2,192,512]{2,1,0:T(8,128)(2,1)S(1)}, u32[]{:S(2)}, u32[]{:S(2)}) %collective-permute-start.24) | collective-permute-done | bytes 393248 | tf_op jit(solution)/shard_map/ppermute | solution.py:239
  47.4 2.7 shard_map.93
  50.1 2.8 shard_map.94
  56.6 3.1 %collective-permute-start.16 = (bf16[2,192,512]{2,1,0:T(8,128)(2,1)}, bf16[2,192,512]{2,1,0:T(8,128)(2,1)S(1)}, u32[]{:S(2)}, u32[]{:S(2)}) collective-permute-start(bf16[2,192,512]{2,1,0:T(8,128)(2,1)} %shard_map.93), channel_id=1, source_target_pairs={{0,3},{1,2},{2,1},{3,0},{4,7},{5,6},{6,5},{7,4},{8,11},{9,10},{10,... | collective-permute-start | bytes 1179656 | tf_op jit(solution)/shard_map/ppermute | solution.py:239
  61.9 2.7 shard_map.96
  64.6 12.6 %collective-permute-done.28.refs_5_ = bf16[2,192,512]{2,1,0:T(8,128)(2,1)S(1)} collective-permute-done((bf16[2,192,512]{2,1,0:T(8,128)(2,1)}, bf16[2,192,512]{2,1,0:T(8,128)(2,1)S(1)}, u32[]{:S(2)}, u32[]{:S(2)}) %collective-permute-start.28) | collective-permute-done | bytes 393248 | tf_op jit(solution)/shard_map/ppermute | solution.py:239
  82.0 2.8 shard_map.98
  84.8 2.7 shard_map.99
  87.5 8.4 %collective-permute-done.30.refs_7_ = bf16[2,192,512]{2,1,0:T(8,128)(2,1)S(1)} collective-permute-done((bf16[2,192,512]{2,1,0:T(8,128)(2,1)S(1)}, bf16[2,192,512]{2,1,0:T(8,128)(2,1)S(1)}, u32[]{:S(2)}, u32[]{:S(2)}) %collective-permute-start.30) | collective-permute-done | bytes 393248 | tf_op jit(solution)/shard_map/ppermute | solution.py:239
  95.9 2.7 shard_map.100
  98.9 3.6 %collective-permute-done.17.refs_1_ = bf16[2,192,512]{2,1,0:T(8,128)(2,1)S(1)} collective-permute-done((bf16[2,192,512]{2,1,0:T(8,128)(2,1)}, bf16[2,192,512]{2,1,0:T(8,128)(2,1)S(1)}, u32[]{:S(2)}, u32[]{:S(2)}) %collective-permute-start.17) | collective-permute-done | bytes 393248 | tf_op jit(solution)/shard_map/ppermute | solution.py:239
  102.5 11.0 %collective-permute-start.22 = (bf16[2,192,512]{2,1,0:T(8,128)(2,1)S(1)}, bf16[2,192,512]{2,1,0:T(8,128)(2,1)S(1)}, u32[]{:S(2)}, u32[]{:S(2)}) collective-permute-start(bf16[2,192,512]{2,1,0:T(8,128)(2,1)S(1)} %copy-done.30), channel_id=1, source_target_pairs={{0,1},{1,0},{2,3},{3,2},{4,5},{5,4},{6,7},{7,6},{8,9},{9,8},{10,11... | collective-permute-start | bytes 1179656 | tf_op jit(solution)/shard_map/ppermute | solution.py:239
  113.5 2.7 shard_map.87
  116.3 13.3 %collective-permute-done.19.refs_3_ = bf16[2,192,512]{2,1,0:T(8,128)(2,1)S(1)} collective-permute-done((bf16[2,192,512]{2,1,0:T(8,128)(2,1)}, bf16[2,192,512]{2,1,0:T(8,128)(2,1)S(1)}, u32[]{:S(2)}, u32[]{:S(2)}) %collective-permute-start.19) | collective-permute-done | bytes 393248 | tf_op jit(solution)/shard_map/ppermute | solution.py:239
  129.7 3.4 %collective-permute-start.10 = (bf16[2,192,512]{2,1,0:T(8,128)(2,1)}, bf16[2,192,512]{2,1,0:T(8,128)(2,1)S(1)}, u32[]{:S(2)}, u32[]{:S(2)}) collective-permute-start(bf16[2,192,512]{2,1,0:T(8,128)(2,1)} %shard_map.87), channel_id=1, source_target_pairs={{0,15},{1,30},{2,13},{3,28},{4,11},{5,26},{6,9},{7,24},{8,23},{9,6... | collective-permute-start | bytes 1179656 | tf_op jit(solution)/shard_map/ppermute | solution.py:239
  133.1 2.7 shard_map.88
  135.8 2.7 shard_map.89
  138.5 2.7 shard_map.90
  141.3 2.7 shard_map.91
  146.6 2.7 shard_map.92
  149.3 6.5 %collective-permute-done.23.refs_7_ = bf16[2,192,512]{2,1,0:T(8,128)(2,1)S(1)} collective-permute-done((bf16[2,192,512]{2,1,0:T(8,128)(2,1)S(1)}, bf16[2,192,512]{2,1,0:T(8,128)(2,1)S(1)}, u32[]{:S(2)}, u32[]{:S(2)}) %collective-permute-start.23) | collective-permute-done | bytes 393248 | tf_op jit(solution)/shard_map/ppermute | solution.py:239
  155.8 5.0 %collective-permute-start.14 = (bf16[2,192,512]{2,1,0:T(8,128)(2,1)}, bf16[2,192,512]{2,1,0:T(8,128)(2,1)S(1)}, u32[]{:S(2)}, u32[]{:S(2)}) collective-permute-start(bf16[2,192,512]{2,1,0:T(8,128)(2,1)} %shard_map.91), channel_id=1, source_target_pairs={{0,11},{1,26},{2,9},{3,24},{4,15},{5,30},{6,13},{7,28},{8,19},{9,2... | collective-permute-start | bytes 1179656 | tf_op jit(solution)/shard_map/ppermute | solution.py:239
  160.7 14.0 %collective-permute-start.15 = (bf16[2,192,512]{2,1,0:T(8,128)(2,1)}, bf16[2,192,512]{2,1,0:T(8,128)(2,1)S(1)}, u32[]{:S(2)}, u32[]{:S(2)}) collective-permute-start(bf16[2,192,512]{2,1,0:T(8,128)(2,1)} %shard_map.92), channel_id=1, source_target_pairs={{0,27},{1,10},{2,25},{3,8},{4,31},{5,14},{6,29},{7,12},{8,3},{9,18... | collective-permute-start | bytes 1179656 | tf_op jit(solution)/shard_map/ppermute | solution.py:239
  177.4 2.7 shard_map.86
  180.1 2.7 shard_map.81
  182.8 3.2 %collective-permute-start.8 = (bf16[2,192,512]{2,1,0:T(8,128)(2,1)}, bf16[2,192,512]{2,1,0:T(8,128)(2,1)S(1)}, u32[]{:S(2)}, u32[]{:S(2)}) collective-permute-start(bf16[2,192,512]{2,1,0:T(8,128)(2,1)} %shard_map.85), channel_id=1, source_target_pairs={{0,14},{1,31},{2,12},{3,29},{4,10},{5,27},{6,8},{7,25},{8,22},{9,7... | collective-permute-start | bytes 1179656 | tf_op jit(solution)/shard_map/ppermute | solution.py:239
  188.9 5.2 %collective-permute-start.4 = (bf16[2,192,512]{2,1,0:T(8,128)(2,1)S(1)}, bf16[2,192,512]{2,1,0:T(8,128)(2,1)S(1)}, u32[]{:S(2)}, u32[]{:S(2)}) collective-permute-start(bf16[2,192,512]{2,1,0:T(8,128)(2,1)S(1)} %copy-done.32), channel_id=1, source_target_pairs={{0,12},{1,29},{2,14},{3,31},{4,8},{5,25},{6,10},{7,27},{8,20},{9,5... | collective-permute-start | bytes 1179656 | tf_op jit(solution)/shard_map/ppermute | solution.py:239
  194.1 2.7 shard_map.83
  196.8 6.8 %collective-permute-start.5 = (bf16[2,192,512]{2,1,0:T(8,128)(2,1)}, bf16[2,192,512]{2,1,0:T(8,128)(2,1)}, u32[]{:S(2)}, u32[]{:S(2)}) collective-permute-start(bf16[2,192,512]{2,1,0:T(8,128)(2,1)} %shard_map.82), channel_id=1, source_target_pairs={{0,28},{1,13},{2,30},{3,15},{4,24},{5,9},{6,26},{7,11},{8,4},{9,21... | collective-permute-start | bytes 1179656 | tf_op jit(solution)/shard_map/ppermute | solution.py:239
  204.3 4.6 %collective-permute-start.6 = (bf16[2,192,512]{2,1,0:T(8,128)(2,1)}, bf16[2,192,512]{2,1,0:T(8,128)(2,1)}, u32[]{:S(2)}, u32[]{:S(2)}) collective-permute-start(bf16[2,192,512]{2,1,0:T(8,128)(2,1)} %shard_map.83), channel_id=1, source_target_pairs={{0,13},{1,28},{2,15},{3,30},{4,9},{5,24},{6,11},{7,26},{8,21},{9,4... | collective-permute-start | bytes 1179656 | tf_op jit(solution)/shard_map/ppermute | solution.py:239
  208.9 2.7 shard_map.84
  211.6 2.7 shard_map.79
  217.0 4.6 %collective-permute-done.8.refs_0_ = bf16[2,192,512]{2,1,0:T(8,128)(2,1)S(1)} collective-permute-done((bf16[2,192,512]{2,1,0:T(8,128)(2,1)}, bf16[2,192,512]{2,1,0:T(8,128)(2,1)S(1)}, u32[]{:S(2)}, u32[]{:S(2)}) %collective-permute-start.8) | collective-permute-done | bytes 393248 | tf_op jit(solution)/shard_map/ppermute | solution.py:239
  223.1 2.7 shard_map.77
  225.9 5.5 %collective-permute-done.4.refs_0_ = bf16[2,192,512]{2,1,0:T(8,128)(2,1)S(1)} collective-permute-done((bf16[2,192,512]{2,1,0:T(8,128)(2,1)S(1)}, bf16[2,192,512]{2,1,0:T(8,128)(2,1)S(1)}, u32[]{:S(2)}, u32[]{:S(2)}) %collective-permute-start.4) | collective-permute-done | bytes 393248 | tf_op jit(solution)/shard_map/ppermute | solution.py:239
  231.4 12.4 %collective-permute-start.3 = (bf16[2,192,512]{2,1,0:T(8,128)(2,1)S(1)}, bf16[2,192,512]{2,1,0:T(8,128)(2,1)S(1)}, u32[]{:S(2)}, u32[]{:S(2)}) collective-permute-start(bf16[2,192,512]{2,1,0:T(8,128)(2,1)S(1)} %copy-done.28), channel_id=1, source_target_pairs={{0,24},{1,9},{2,26},{3,11},{4,28},{5,13},{6,30},{7,15},{8,0},{9,17... | collective-permute-start | bytes 1179656 | tf_op jit(solution)/shard_map/ppermute | solution.py:239
  246.6 14.3 %collective-permute-start.1 = (bf16[2,192,512]{2,1,0:T(8,128)(2,1)}, bf16[2,192,512]{2,1,0:T(8,128)(2,1)S(1)}, u32[]{:S(2)}, u32[]{:S(2)}) collective-permute-start(bf16[2,192,512]{2,1,0:T(8,128)(2,1)} %shard_map.78), channel_id=1, source_target_pairs={{0,25},{1,8},{2,27},{3,10},{4,29},{5,12},{6,31},{7,14},{8,1},{9,16... | collective-permute-start | bytes 1179656 | tf_op jit(solution)/shard_map/ppermute | solution.py:239
  264.4 4.8 %shard_map.109 = (bf16[2,192,16384]{2,1,0:T(8,128)(2,1)}, f32[2,192,512]{2,1,0:T(8,128)}) custom-call(s32[32]{0:T(128)} %select_reduce_fusion.2.spot_ref, bf16[2,192,512]{2,1,0:T(8,128)(2,1)} %shard_map.101.refs_0_, bf16[2,192,512]{2,1,0:T(8,128)(2,1)} %copy-done.4, bf16[2,192,512]{2,1,0:T(8,128)(2,1)} %copy-done.5, bf16[2,192,512]{2,1,0:T(8,128)(2,1)} %copy-done.6, ...), custom_call_target="tpu_custom_call" | custom-call | tf_op jit(solution)/shard_map/pallas_call | solution.py:183
  269.2 5.9 %shard_map.110 = (bf16[2,192,16384]{2,1,0:T(8,128)(2,1)}, f32[2,192,512]{2,1,0:T(8,128)}) custom-call(s32[32]{0:T(128)} %select_reduce_fusion.2.spot_ref, bf16[2,192,512]{2,1,0:T(8,128)(2,1)} %copy-done.11, bf16[2,192,512]{2,1,0:T(8,128)(2,1)} %copy-done.12, bf16[2,192,512]{2,1,0:T(8,128)(2,1)} %copy-done.13, ...), custom_call_target="tpu_custom_call", output_to_operand_aliasing={{0}: (9, {}), {1}: (10, {})} | custom-call | tf_op jit(solution)/shard_map/pallas_call | solution.py:183
  275.1 5.9 %shard_map.111 = (bf16[2,192,16384]{2,1,0:T(8,128)(2,1)}, f32[2,192,512]{2,1,0:T(8,128)}) custom-call(s32[32]{0:T(128)} %select_reduce_fusion.2.spot_ref, bf16[2,192,512]{2,1,0:T(8,128)(2,1)} %copy-done.25, bf16[2,192,512]{2,1,0:T(8,128)(2,1)} %collective-permute-done.9.refs_1_, ...), custom_call_target="tpu_custom_call", output_to_operand_aliasing={{0}: (9, {}), {1}: (10, {})} | custom-call | tf_op jit(solution)/shard_map/pallas_call | solution.py:183
  281.1 4.3 %shard_map.112 = (bf16[2,192,16384]{2,1,0:T(8,128)(2,1)}, f32[2,192,512]{2,1,0:T(8,128)}) custom-call(s32[32]{0:T(128)} %select_reduce_fusion.2.spot_ref, bf16[2,192,512]{2,1,0:T(8,128)(2,1)} %copy-done.26, bf16[2,192,512]{2,1,0:T(8,128)(2,1)} %collective-permute-done.5.refs_1_, ...), custom_call_target="tpu_custom_call", output_to_operand_aliasing={{0}: (5, {}), {1}: (6, {})} | custom-call | tf_op jit(solution)/shard_map/pallas_call | solution.py:183
  286.3 3.5 %shard_map.113 = (bf16[2,192,16384]{2,1,0:T(8,128)(2,1)}, f32[2,192,512]{2,1,0:T(8,128)}) custom-call(s32[32]{0:T(128)} %select_reduce_fusion.2.spot_ref, bf16[2,192,512]{2,1,0:T(8,128)(2,1)} %copy-done, bf16[2,192,512]{2,1,0:T(8,128)(2,1)} %copy-done.2, ...), custom_call_target="tpu_custom_call", output_to_operand_aliasing={{0}: (3, {}), {1}: (4, {})} | custom-call | tf_op jit(solution)/shard_map/pallas_call | solution.py:183
  290.8 3.5 %shard_map.114 = (bf16[2,192,16384]{2,1,0:T(8,128)(2,1)}, f32[2,192,512]{2,1,0:T(8,128)}) custom-call(s32[32]{0:T(128)} %select_reduce_fusion.2.spot_ref, bf16[2,192,512]{2,1,0:T(8,128)(2,1)} %copy-done.1, bf16[2,192,512]{2,1,0:T(8,128)(2,1)} %copy-done.3, ...), custom_call_target="tpu_custom_call", output_to_operand_aliasing={{0}: (3, {}), {1}: (4, {})} | custom-call | tf_op jit(solution)/shard_map/pallas_call | solution.py:183
  (130 shorter events, 49.8 us)
Async XLA Ops:
  6.2 38.2 %collective-permute-start.24 = (bf16[2,192,512]{2,1,0:T(8,128)(2,1)}, bf16[2,192,512]{2,1,0:T(8,128)(2,1)S(1)}, u32[]{:S(2)}, u32[]{:S(2)}) collective-permute-start(bf16[2,192,512]{2,1,0:T(8,128)(2,1)} %shard_map.102), channel_id=1, source_target_pairs={{0,22},{1,23},{2,20},{3,21},{4,18},{5,19},{6,16},{7,17},{8,30},{9,... | collective-permute-start | bytes 1179656 | tf_op jit(solution)/shard_map/ppermute | solution.py:239
  11.1 41.8 %collective-permute-start.25 = (bf16[2,192,512]{2,1,0:T(8,128)(2,1)}, bf16[2,192,512]{2,1,0:T(8,128)(2,1)S(1)}, u32[]{:S(2)}, u32[]{:S(2)}) collective-permute-start(bf16[2,192,512]{2,1,0:T(8,128)(2,1)} %shard_map.103), channel_id=1, source_target_pairs={{0,6},{1,7},{2,4},{3,5},{4,2},{5,3},{6,0},{7,1},{8,14},{9,15},{10,... | collective-permute-start | bytes 1179656 | tf_op jit(solution)/shard_map/ppermute | solution.py:239
  16.0 40.7 %collective-permute-start.26 = (bf16[2,192,512]{2,1,0:T(8,128)(2,1)}, bf16[2,192,512]{2,1,0:T(8,128)(2,1)S(1)}, u32[]{:S(2)}, u32[]{:S(2)}) collective-permute-start(bf16[2,192,512]{2,1,0:T(8,128)(2,1)} %shard_map.104), channel_id=1, source_target_pairs={{0,23},{1,22},{2,21},{3,20},{4,19},{5,18},{6,17},{7,16},{8,31},{9,... | collective-permute-start | bytes 1179656 | tf_op jit(solution)/shard_map/ppermute | solution.py:239
  19.5 40.2 %collective-permute-start.27 = (bf16[2,192,512]{2,1,0:T(8,128)(2,1)}, bf16[2,192,512]{2,1,0:T(8,128)(2,1)S(1)}, u32[]{:S(2)}, u32[]{:S(2)}) collective-permute-start(bf16[2,192,512]{2,1,0:T(8,128)(2,1)} %shard_map.105), channel_id=1, source_target_pairs={{0,7},{1,6},{2,5},{3,4},{4,3},{5,2},{6,1},{7,0},{8,15},{9,14},{10,... | collective-permute-start | bytes 1179656 | tf_op jit(solution)/shard_map/ppermute | solution.py:239
  23.8 53.4 %collective-permute-start.28 = (bf16[2,192,512]{2,1,0:T(8,128)(2,1)}, bf16[2,192,512]{2,1,0:T(8,128)(2,1)S(1)}, u32[]{:S(2)}, u32[]{:S(2)}) collective-permute-start(bf16[2,192,512]{2,1,0:T(8,128)(2,1)} %shard_map.106), channel_id=1, source_target_pairs={{0,18},{1,19},{2,16},{3,17},{4,22},{5,23},{6,20},{7,21},{8,26},{9,... | collective-permute-start | bytes 1179656 | tf_op jit(solution)/shard_map/ppermute | solution.py:239
  44.4 34.0 %collective-permute-start.29 = (bf16[2,192,512]{2,1,0:T(8,128)(2,1)}, bf16[2,192,512]{2,1,0:T(8,128)(2,1)S(1)}, u32[]{:S(2)}, u32[]{:S(2)}) collective-permute-start(bf16[2,192,512]{2,1,0:T(8,128)(2,1)} %shard_map.107), channel_id=1, source_target_pairs={{0,2},{1,3},{2,0},{3,1},{4,6},{5,7},{6,4},{7,5},{8,10},{9,11},{10,... | collective-permute-start | bytes 1179656 | tf_op jit(solution)/shard_map/ppermute | solution.py:239
  52.9 43.0 %collective-permute-start.30 = (bf16[2,192,512]{2,1,0:T(8,128)(2,1)S(1)}, bf16[2,192,512]{2,1,0:T(8,128)(2,1)S(1)}, u32[]{:S(2)}, u32[]{:S(2)}) collective-permute-start(bf16[2,192,512]{2,1,0:T(8,128)(2,1)S(1)} %copy-done.33), channel_id=1, source_target_pairs={{0,19},{1,18},{2,17},{3,16},{4,23},{5,22},{6,21},{7,20},{8,27},{9,... | collective-permute-start | bytes 1179656 | tf_op jit(solution)/shard_map/ppermute | solution.py:239
  56.6 7.9 %copy-start.6 = (bf16[2,192,512]{2,1,0:T(8,128)(2,1)}, bf16[2,192,512]{2,1,0:T(8,128)(2,1)S(1)}, u32[]{:S(2)}) copy-start(bf16[2,192,512]{2,1,0:T(8,128)(2,1)S(1)} %collective-permute-done.26.refs_3_) | copy-start | bytes 1179652
  56.6 42.0 %collective-permute-start.16 = (bf16[2,192,512]{2,1,0:T(8,128)(2,1)}, bf16[2,192,512]{2,1,0:T(8,128)(2,1)S(1)}, u32[]{:S(2)}, u32[]{:S(2)}) collective-permute-start(bf16[2,192,512]{2,1,0:T(8,128)(2,1)} %shard_map.93), channel_id=1, source_target_pairs={{0,3},{1,2},{2,1},{3,0},{4,7},{5,6},{6,5},{7,4},{8,11},{9,10},{10,... | collective-permute-start | bytes 1179656 | tf_op jit(solution)/shard_map/ppermute | solution.py:239
  59.8 42.7 %collective-permute-start.17 = (bf16[2,192,512]{2,1,0:T(8,128)(2,1)}, bf16[2,192,512]{2,1,0:T(8,128)(2,1)S(1)}, u32[]{:S(2)}, u32[]{:S(2)}) collective-permute-start(bf16[2,192,512]{2,1,0:T(8,128)(2,1)} %shard_map.94), channel_id=1, source_target_pairs={{0,20},{1,21},{2,22},{3,23},{4,16},{5,17},{6,18},{7,19},{8,28},{9,... | collective-permute-start | bytes 1179656 | tf_op jit(solution)/shard_map/ppermute | solution.py:239
  77.2 39.1 %collective-permute-start.18 = (bf16[2,192,512]{2,1,0:T(8,128)(2,1)}, bf16[2,192,512]{2,1,0:T(8,128)(2,1)S(1)}, u32[]{:S(2)}, u32[]{:S(2)}) collective-permute-start(bf16[2,192,512]{2,1,0:T(8,128)(2,1)} %shard_map.95), channel_id=1, source_target_pairs={{0,4},{1,5},{2,6},{3,7},{4,0},{5,1},{6,2},{7,3},{8,12},{9,13},{10,... | collective-permute-start | bytes 1179656 | tf_op jit(solution)/shard_map/ppermute | solution.py:239
  78.4 51.3 %collective-permute-start.19 = (bf16[2,192,512]{2,1,0:T(8,128)(2,1)}, bf16[2,192,512]{2,1,0:T(8,128)(2,1)S(1)}, u32[]{:S(2)}, u32[]{:S(2)}) collective-permute-start(bf16[2,192,512]{2,1,0:T(8,128)(2,1)} %shard_map.96), channel_id=1, source_target_pairs={{0,21},{1,20},{2,23},{3,22},{4,17},{5,16},{6,19},{7,18},{8,29},{9,... | collective-permute-start | bytes 1179656 | tf_op jit(solution)/shard_map/ppermute | solution.py:239
  87.5 15.0 %copy-start.30 = (bf16[2,192,512]{2,1,0:T(8,128)(2,1)S(1)}, bf16[2,192,512]{2,1,0:T(8,128)(2,1)}, u32[]{:S(2)}) copy-start(bf16[2,192,512]{2,1,0:T(8,128)(2,1)} %shard_map.99) | copy-start | bytes 1179652
  95.9 45.3 %collective-permute-start.20 = (bf16[2,192,512]{2,1,0:T(8,128)(2,1)}, bf16[2,192,512]{2,1,0:T(8,128)(2,1)S(1)}, u32[]{:S(2)}, u32[]{:S(2)}) collective-permute-start(bf16[2,192,512]{2,1,0:T(8,128)(2,1)} %shard_map.97), channel_id=1, source_target_pairs={{0,5},{1,4},{2,7},{3,6},{4,1},{5,0},{6,3},{7,2},{8,13},{9,12},{10,... | collective-permute-start | bytes 1179656 | tf_op jit(solution)/shard_map/ppermute | solution.py:239
  98.7 17.6 %copy-start.31 = (bf16[2,192,512]{2,1,0:T(8,128)(2,1)S(1)}, bf16[2,192,512]{2,1,0:T(8,128)(2,1)}, u32[]{:S(2)}) copy-start(bf16[2,192,512]{2,1,0:T(8,128)(2,1)} %shard_map.100) | copy-start | bytes 1179652
  98.7 17.5 %copy-start.11 = (bf16[2,192,512]{2,1,0:T(8,128)(2,1)}, bf16[2,192,512]{2,1,0:T(8,128)(2,1)S(1)}, u32[]{:S(2)}) copy-start(bf16[2,192,512]{2,1,0:T(8,128)(2,1)S(1)} %collective-permute-done.16.refs_0_) | copy-start | bytes 1179652
  98.7 45.4 %collective-permute-start.21 = (bf16[2,192,512]{2,1,0:T(8,128)(2,1)}, bf16[2,192,512]{2,1,0:T(8,128)(2,1)S(1)}, u32[]{:S(2)}, u32[]{:S(2)}) collective-permute-start(bf16[2,192,512]{2,1,0:T(8,128)(2,1)} %shard_map.98), channel_id=1, source_target_pairs={{0,16},{1,17},{2,18},{3,19},{4,20},{5,21},{6,22},{7,23},{8,24},{9,... | collective-permute-start | bytes 1179656 | tf_op jit(solution)/shard_map/ppermute | solution.py:239
  102.5 13.7 %copy-start.12 = (bf16[2,192,512]{2,1,0:T(8,128)(2,1)}, bf16[2,192,512]{2,1,0:T(8,128)(2,1)S(1)}, u32[]{:S(2)}) copy-start(bf16[2,192,512]{2,1,0:T(8,128)(2,1)S(1)} %collective-permute-done.17.refs_1_) | copy-start | bytes 1179652
  102.5 43.1 %collective-permute-start.22 = (bf16[2,192,512]{2,1,0:T(8,128)(2,1)S(1)}, bf16[2,192,512]{2,1,0:T(8,128)(2,1)S(1)}, u32[]{:S(2)}, u32[]{:S(2)}) collective-permute-start(bf16[2,192,512]{2,1,0:T(8,128)(2,1)S(1)} %copy-done.30), channel_id=1, source_target_pairs={{0,1},{1,0},{2,3},{3,2},{4,5},{5,4},{6,7},{7,6},{8,9},{9,8},{10,11... | collective-permute-start | bytes 1179656 | tf_op jit(solution)/shard_map/ppermute | solution.py:239
  116.2 19.6 %copy-start.13 = (bf16[2,192,512]{2,1,0:T(8,128)(2,1)}, bf16[2,192,512]{2,1,0:T(8,128)(2,1)S(1)}, u32[]{:S(2)}) copy-start(bf16[2,192,512]{2,1,0:T(8,128)(2,1)S(1)} %collective-permute-done.18.refs_2_) | copy-start | bytes 1179652
  116.2 39.5 %collective-permute-start.23 = (bf16[2,192,512]{2,1,0:T(8,128)(2,1)S(1)}, bf16[2,192,512]{2,1,0:T(8,128)(2,1)S(1)}, u32[]{:S(2)}, u32[]{:S(2)}) collective-permute-start(bf16[2,192,512]{2,1,0:T(8,128)(2,1)S(1)} %copy-done.31), channel_id=1, source_target_pairs={{0,17},{1,16},{2,19},{3,18},{4,21},{5,20},{6,23},{7,22},{8,25},{9,... | collective-permute-start | bytes 1179656 | tf_op jit(solution)/shard_map/ppermute | solution.py:239
  129.7 31.1 %collective-permute-start.10 = (bf16[2,192,512]{2,1,0:T(8,128)(2,1)}, bf16[2,192,512]{2,1,0:T(8,128)(2,1)S(1)}, u32[]{:S(2)}, u32[]{:S(2)}) collective-permute-start(bf16[2,192,512]{2,1,0:T(8,128)(2,1)} %shard_map.87), channel_id=1, source_target_pairs={{0,15},{1,30},{2,13},{3,28},{4,11},{5,26},{6,9},{7,24},{8,23},{9,6... | collective-permute-start | bytes 1179656 | tf_op jit(solution)/shard_map/ppermute | solution.py:239
  141.2 41.6 %collective-permute-start.11 = (bf16[2,192,512]{2,1,0:T(8,128)(2,1)}, bf16[2,192,512]{2,1,0:T(8,128)(2,1)S(1)}, u32[]{:S(2)}, u32[]{:S(2)}) collective-permute-start(bf16[2,192,512]{2,1,0:T(8,128)(2,1)} %shard_map.88), channel_id=1, source_target_pairs={{0,31},{1,14},{2,29},{3,12},{4,27},{5,10},{6,25},{7,8},{8,7},{9,22... | collective-permute-start | bytes 1179656 | tf_op jit(solution)/shard_map/ppermute | solution.py:239
  144.1 44.6 %collective-permute-start.12 = (bf16[2,192,512]{2,1,0:T(8,128)(2,1)}, bf16[2,192,512]{2,1,0:T(8,128)(2,1)S(1)}, u32[]{:S(2)}, u32[]{:S(2)}) collective-permute-start(bf16[2,192,512]{2,1,0:T(8,128)(2,1)} %shard_map.89), channel_id=1, source_target_pairs={{0,10},{1,27},{2,8},{3,25},{4,14},{5,31},{6,12},{7,29},{8,18},{9,3... | collective-permute-start | bytes 1179656 | tf_op jit(solution)/shard_map/ppermute | solution.py:239
  145.5 43.4 %collective-permute-start.13 = (bf16[2,192,512]{2,1,0:T(8,128)(2,1)}, bf16[2,192,512]{2,1,0:T(8,128)(2,1)S(1)}, u32[]{:S(2)}, u32[]{:S(2)}) collective-permute-start(bf16[2,192,512]{2,1,0:T(8,128)(2,1)} %shard_map.90), channel_id=1, source_target_pairs={{0,26},{1,11},{2,24},{3,9},{4,30},{5,15},{6,28},{7,13},{8,2},{9,19... | collective-permute-start | bytes 1179656 | tf_op jit(solution)/shard_map/ppermute | solution.py:239
  155.8 21.6 %copy-start.18 = (bf16[2,192,512]{2,1,0:T(8,128)(2,1)}, bf16[2,192,512]{2,1,0:T(8,128)(2,1)S(1)}, u32[]{:S(2)}) copy-start(bf16[2,192,512]{2,1,0:T(8,128)(2,1)S(1)} %collective-permute-done.23.refs_7_) | copy-start | bytes 1179652
  155.8 41.1 %collective-permute-start.14 = (bf16[2,192,512]{2,1,0:T(8,128)(2,1)}, bf16[2,192,512]{2,1,0:T(8,128)(2,1)S(1)}, u32[]{:S(2)}, u32[]{:S(2)}) collective-permute-start(bf16[2,192,512]{2,1,0:T(8,128)(2,1)} %shard_map.91), channel_id=1, source_target_pairs={{0,11},{1,26},{2,9},{3,24},{4,15},{5,30},{6,13},{7,28},{8,19},{9,2... | collective-permute-start | bytes 1179656 | tf_op jit(solution)/shard_map/ppermute | solution.py:239
  160.7 16.7 %copy-start.19 = (bf16[2,192,512]{2,1,0:T(8,128)(2,1)}, bf16[2,192,512]{2,1,0:T(8,128)(2,1)S(1)}, u32[]{:S(2)}) copy-start(bf16[2,192,512]{2,1,0:T(8,128)(2,1)S(1)} %collective-permute-done.10.refs_2_) | copy-start | bytes 1179652
  160.7 43.6 %collective-permute-start.15 = (bf16[2,192,512]{2,1,0:T(8,128)(2,1)}, bf16[2,192,512]{2,1,0:T(8,128)(2,1)S(1)}, u32[]{:S(2)}, u32[]{:S(2)}) collective-permute-start(bf16[2,192,512]{2,1,0:T(8,128)(2,1)} %shard_map.92), channel_id=1, source_target_pairs={{0,27},{1,10},{2,25},{3,8},{4,31},{5,14},{6,29},{7,12},{8,3},{9,18... | collective-permute-start | bytes 1179656 | tf_op jit(solution)/shard_map/ppermute | solution.py:239
  182.8 38.8 %collective-permute-start.8 = (bf16[2,192,512]{2,1,0:T(8,128)(2,1)}, bf16[2,192,512]{2,1,0:T(8,128)(2,1)S(1)}, u32[]{:S(2)}, u32[]{:S(2)}) collective-permute-start(bf16[2,192,512]{2,1,0:T(8,128)(2,1)} %shard_map.85), channel_id=1, source_target_pairs={{0,14},{1,31},{2,12},{3,29},{4,10},{5,27},{6,8},{7,25},{8,22},{9,7... | collective-permute-start | bytes 1179656 | tf_op jit(solution)/shard_map/ppermute | solution.py:239
  188.7 8.1 %copy-start.21 = (bf16[2,192,512]{2,1,0:T(8,128)(2,1)}, bf16[2,192,512]{2,1,0:T(8,128)(2,1)S(1)}, u32[]{:S(2)}) copy-start(bf16[2,192,512]{2,1,0:T(8,128)(2,1)S(1)} %collective-permute-done.12.refs_4_) | copy-start | bytes 1179652
  188.7 37.1 %collective-permute-start.9 = (bf16[2,192,512]{2,1,0:T(8,128)(2,1)}, bf16[2,192,512]{2,1,0:T(8,128)(2,1)}, u32[]{:S(2)}, u32[]{:S(2)}) collective-permute-start(bf16[2,192,512]{2,1,0:T(8,128)(2,1)} %shard_map.86), channel_id=1, source_target_pairs={{0,30},{1,15},{2,28},{3,13},{4,26},{5,11},{6,24},{7,9},{8,6},{9,23... | collective-permute-start | bytes 1179656 | tf_op jit(solution)/shard_map/ppermute | solution.py:239
  188.9 7.9 %copy-start.22 = (bf16[2,192,512]{2,1,0:T(8,128)(2,1)}, bf16[2,192,512]{2,1,0:T(8,128)(2,1)S(1)}, u32[]{:S(2)}) copy-start(bf16[2,192,512]{2,1,0:T(8,128)(2,1)S(1)} %collective-permute-done.13.refs_5_) | copy-start | bytes 1179652
  188.9 42.5 %collective-permute-start.4 = (bf16[2,192,512]{2,1,0:T(8,128)(2,1)S(1)}, bf16[2,192,512]{2,1,0:T(8,128)(2,1)S(1)}, u32[]{:S(2)}, u32[]{:S(2)}) collective-permute-start(bf16[2,192,512]{2,1,0:T(8,128)(2,1)S(1)} %copy-done.32), channel_id=1, source_target_pairs={{0,12},{1,29},{2,14},{3,31},{4,8},{5,25},{6,10},{7,27},{8,20},{9,5... | collective-permute-start | bytes 1179656 | tf_op jit(solution)/shard_map/ppermute | solution.py:239
  196.8 14.8 %copy-start.23 = (bf16[2,192,512]{2,1,0:T(8,128)(2,1)}, bf16[2,192,512]{2,1,0:T(8,128)(2,1)S(1)}, u32[]{:S(2)}) copy-start(bf16[2,192,512]{2,1,0:T(8,128)(2,1)S(1)} %collective-permute-done.14.refs_6_) | copy-start | bytes 1179652
  196.8 49.7 %collective-permute-start.5 = (bf16[2,192,512]{2,1,0:T(8,128)(2,1)}, bf16[2,192,512]{2,1,0:T(8,128)(2,1)}, u32[]{:S(2)}, u32[]{:S(2)}) collective-permute-start(bf16[2,192,512]{2,1,0:T(8,128)(2,1)} %shard_map.82), channel_id=1, source_target_pairs={{0,28},{1,13},{2,30},{3,15},{4,24},{5,9},{6,26},{7,11},{8,4},{9,21... | collective-permute-start | bytes 1179656 | tf_op jit(solution)/shard_map/ppermute | solution.py:239
  204.3 42.3 %collective-permute-start.6 = (bf16[2,192,512]{2,1,0:T(8,128)(2,1)}, bf16[2,192,512]{2,1,0:T(8,128)(2,1)}, u32[]{:S(2)}, u32[]{:S(2)}) collective-permute-start(bf16[2,192,512]{2,1,0:T(8,128)(2,1)} %shard_map.83), channel_id=1, source_target_pairs={{0,13},{1,28},{2,15},{3,30},{4,9},{5,24},{6,11},{7,26},{8,21},{9,4... | collective-permute-start | bytes 1179656 | tf_op jit(solution)/shard_map/ppermute | solution.py:239
  217.0 8.8 %copy-start.29 = (bf16[2,192,512]{2,1,0:T(8,128)(2,1)S(1)}, bf16[2,192,512]{2,1,0:T(8,128)(2,1)}, u32[]{:S(2)}) copy-start(bf16[2,192,512]{2,1,0:T(8,128)(2,1)} %shard_map.79) | copy-start | bytes 1179652
  217.0 14.4 %copy-start.28 = (bf16[2,192,512]{2,1,0:T(8,128)(2,1)S(1)}, bf16[2,192,512]{2,1,0:T(8,128)(2,1)}, u32[]{:S(2)}) copy-start(bf16[2,192,512]{2,1,0:T(8,128)(2,1)} %shard_map.80) | copy-start | bytes 1179652
  221.6 59.4 %collective-permute-start.7 = (bf16[2,192,512]{2,1,0:T(8,128)(2,1)}, bf16[2,192,512]{2,1,0:T(8,128)(2,1)}, u32[]{:S(2)}, u32[]{:S(2)}) collective-permute-start(bf16[2,192,512]{2,1,0:T(8,128)(2,1)} %shard_map.84), channel_id=1, source_target_pairs={{0,29},{1,12},{2,31},{3,14},{4,25},{5,8},{6,27},{7,10},{8,5},{9,20... | collective-permute-start | bytes 1179656 | tf_op jit(solution)/shard_map/ppermute | solution.py:239
  225.8 20.8 %copy-start.27 = (bf16[2,192,512]{2,1,0:T(8,128)(2,1)S(1)}, bf16[2,192,512]{2,1,0:T(8,128)(2,1)}, u32[]{:S(2)}) copy-start(bf16[2,192,512]{2,1,0:T(8,128)(2,1)} %shard_map.77) | copy-start | bytes 1179652
  225.8 59.6 %collective-permute-start.2 = (bf16[2,192,512]{2,1,0:T(8,128)(2,1)S(1)}, bf16[2,192,512]{2,1,0:T(8,128)(2,1)S(1)}, u32[]{:S(2)}, u32[]{:S(2)}) collective-permute-start(bf16[2,192,512]{2,1,0:T(8,128)(2,1)S(1)} %copy-done.29), channel_id=1, source_target_pairs={{0,8},{1,25},{2,10},{3,27},{4,12},{5,29},{6,14},{7,31},{8,16},{9,1... | collective-permute-start | bytes 1179656 | tf_op jit(solution)/shard_map/ppermute | solution.py:239
  231.4 15.1 %copy-start.26 = (bf16[2,192,512]{2,1,0:T(8,128)(2,1)}, bf16[2,192,512]{2,1,0:T(8,128)(2,1)S(1)}, u32[]{:S(2)}) copy-start(bf16[2,192,512]{2,1,0:T(8,128)(2,1)S(1)} %collective-permute-done.4.refs_0_) | copy-start | bytes 1179652
  231.4 54.0 %collective-permute-start.3 = (bf16[2,192,512]{2,1,0:T(8,128)(2,1)S(1)}, bf16[2,192,512]{2,1,0:T(8,128)(2,1)S(1)}, u32[]{:S(2)}, u32[]{:S(2)}) collective-permute-start(bf16[2,192,512]{2,1,0:T(8,128)(2,1)S(1)} %copy-done.28), channel_id=1, source_target_pairs={{0,24},{1,9},{2,26},{3,11},{4,28},{5,13},{6,30},{7,15},{8,0},{9,17... | collective-permute-start | bytes 1179656 | tf_op jit(solution)/shard_map/ppermute | solution.py:239
  246.5 17.1 %copy-start.34 = (s32[31]{0:T(128)S(1)}, s32[31]{0:T(128)}, u32[]{:S(2)}) copy-start(s32[31]{0:T(128)} %get-tuple-element.23) | copy-start | bytes 376
  246.5 17.2 %copy-start.35 = (s32[32]{0:T(128)S(1)}, s32[32]{0:T(128)}, u32[]{:S(2)}) copy-start(s32[32]{0:T(128)} %param.9) | copy-start | bytes 388
  246.6 43.3 %collective-permute-start = (bf16[2,192,512]{2,1,0:T(8,128)(2,1)S(1)}, bf16[2,192,512]{2,1,0:T(8,128)(2,1)S(1)}, u32[]{:S(2)}, u32[]{:S(2)}) collective-permute-start(bf16[2,192,512]{2,1,0:T(8,128)(2,1)S(1)} %copy-done.27), channel_id=1, source_target_pairs={{0,9},{1,24},{2,11},{3,26},{4,13},{5,28},{6,15},{7,30},{8,17},{9,0... | collective-permute-start | bytes 1179656 | tf_op jit(solution)/shard_map/ppermute | solution.py:239
  246.6 43.2 %collective-permute-start.1 = (bf16[2,192,512]{2,1,0:T(8,128)(2,1)}, bf16[2,192,512]{2,1,0:T(8,128)(2,1)S(1)}, u32[]{:S(2)}, u32[]{:S(2)}) collective-permute-start(bf16[2,192,512]{2,1,0:T(8,128)(2,1)} %shard_map.78), channel_id=1, source_target_pairs={{0,25},{1,8},{2,27},{3,10},{4,29},{5,12},{6,31},{7,14},{8,1},{9,16... | collective-permute-start | bytes 1179656 | tf_op jit(solution)/shard_map/ppermute | solution.py:239
  (19 other events, 70.3 us)
